TPU v7x, 32 devices: a whole 2x2x4 slice. The times are simulated.
32 devices in a mesh: dp: 4 (over y, core), seq: 8 (over z, x).
Axes of the slice: x: 2, y: 2, z: 4, core: 2. Of those that a mesh axis runs over, the one named last changes fastest.
Arguments:
- tokens: bfloat16 [32768, 2048], P(('dp', 'seq')), parts along dimension 0, may hold values from -6 to 6
- chosen: int32 [4096], P('dp'), parts along dimension 0, may hold values from 0 to 8191, as said below
- gates: float32 [4096], P('dp'), parts along dimension 0, may hold values from 0.5 to 2
- w_query: bfloat16 [2048, 1024], P('seq'), may hold values from -1.8561553 to 1.8561553
- w_key: bfloat16 [2048, 256], P('seq'), may hold values from -0.088388348 to 0.088388348
- w_value: bfloat16 [2048, 256], P('seq'), may hold values from -0.125 to 0.125
- w_out: bfloat16 [1024, 2048], P(None, 'seq'), may hold values from -0.5 to 0.5
Outputs:
- mixed: bfloat16 [32768, 2048], P(('dp', 'seq')), parts along dimension 0
There are 4 independent parts, one for each index of `dp`. A program takes and returns all parts, laid end to end along the dimension named above; an argument that names none is the same for every part. Nothing has to cross between parts.
Inputs may be any that keep to these rules, and one draw needn't show every extreme that they name: `chosen`: distinct positions in increasing order; at most 256 of them lie in one device's 1024 consecutive positions, and exactly 256 lie in some device's positions.
All inputs are finite; a program needn't handle non-finite values.
Results may differ from a plain program's by a relative error of at most 0.006.
Values may be sent and summed in bfloat16 or wider, within the bound.
A program may use at most 128 MiB of HBM per device.

v0:
```python
import math
import jax
import jax.numpy as jnp
from jax import lax
from jax.sharding import PartitionSpec as P

HEADS = 8
KV_HEADS = 2
HEAD_DIM = 128
ROWS_DEV = 128
MOST_OWN = 256
neg_fill = -1e30


def normalize(row_block):
    widened = row_block.astype(jnp.float32)
    scale_rows = lax.rsqrt(jnp.mean(widened * widened, axis=1, keepdims=True) + 1e-06)
    return (widened * scale_rows).astype(jnp.bfloat16)


def per_device(tokens, chosen, gates, w_query, w_key, w_value, w_out):
    shards = lax.axis_size("seq")
    my_index = lax.axis_index("seq")
    tok_rows = tokens.shape[0]
    model_width = tokens.shape[1]
    picked_total = chosen.shape[0]
    slot_count = (MOST_OWN - 1) // shards + 1
    group_size = HEADS // KV_HEADS
    owner_of = chosen // tok_rows
    owners = jnp.arange(shards, dtype=jnp.int32)
    counts = jnp.sum((owner_of[None, :] == owners[:, None]).astype(jnp.int32), axis=1)
    starts = jnp.cumsum(counts) - counts
    my_start = starts[my_index]
    my_count = counts[my_index]
    my_base = my_index * tok_rows
    own_steps = jnp.arange(MOST_OWN, dtype=jnp.int32)
    own_valid = own_steps < my_count
    slot_steps = jnp.arange(slot_count, dtype=jnp.int32)
    lead_step = (owners - my_start) % shards
    offset = lead_step[:, None] + shards * slot_steps[None, :]
    is_valid = offset < my_count
    flat_ids = jnp.clip((my_start + offset).reshape(-1), 0, picked_total - 1)
    flat_valid = is_valid.reshape(-1)
    spot_row = jnp.where(flat_valid, chosen[flat_ids] - my_base, 0)
    row_block = normalize(tokens[spot_row])
    outgoing = jnp.where(flat_valid[:, None], row_block, jnp.zeros_like(row_block)).reshape(
        shards, slot_count, model_width
    )
    arrived = lax.all_to_all(outgoing, "seq", split_axis=0, concat_axis=0, tiled=True)
    local_rows = jnp.arange(ROWS_DEV, dtype=jnp.int32)
    query_order = my_index + shards * local_rows
    source = owner_of[query_order]
    place_at = source * slot_count + (query_order - starts[source]) // shards
    normed = arrived.reshape(shards * slot_count, model_width)[place_at]

    def key_order_of(row_ids):
        return row_ids // ROWS_DEV + shards * (row_ids % ROWS_DEV)

    rows_here = normed.shape[0]
    pieces = (
        lax.all_gather(w_query, "seq", axis=0, tiled=True),
        lax.all_gather(w_key, "seq", axis=0, tiled=True),
        lax.all_gather(w_value, "seq", axis=0, tiled=True),
    )
    query_sum, key_sum, value_sum = tuple(
        (jnp.dot(normed, piece_now, preferred_element_type=jnp.float32) for piece_now in pieces)
    )
    query_matrix = (
        (query_sum * HEAD_DIM ** (-0.5))
        .astype(jnp.bfloat16)
        .reshape(rows_here, KV_HEADS, group_size, HEAD_DIM)
    )
    keys_all = key_sum.astype(jnp.bfloat16)
    values = value_sum.astype(jnp.bfloat16)
    start_state = (
        jnp.full((KV_HEADS, group_size, rows_here), neg_fill, jnp.float32),
        jnp.zeros((KV_HEADS, group_size, rows_here), jnp.float32),
        jnp.zeros((KV_HEADS, group_size, rows_here, HEAD_DIM), jnp.float32),
    )
    key_rows = lax.all_gather(keys_all, "seq", axis=0, tiled=True)
    value_rows = lax.all_gather(values, "seq", axis=0, tiled=True)
    length = key_rows.shape[0]
    block_rows = math.gcd(length, 512)

    def one_block(step_no, inner_state):
        top_score, weight, mixed_sum = inner_state
        first_row = step_no * block_rows
        key_portion = lax.dynamic_slice_in_dim(key_rows, first_row, block_rows, 0).reshape(
            block_rows, KV_HEADS, HEAD_DIM
        )
        value_piece = lax.dynamic_slice_in_dim(value_rows, first_row, block_rows, 0).reshape(
            block_rows, KV_HEADS, HEAD_DIM
        )
        key_order = key_order_of(first_row + jnp.arange(block_rows, dtype=jnp.int32))
        logit_scores = jnp.einsum(
            "qjfh,ujh->jfqu", query_matrix, key_portion, preferred_element_type=jnp.float32
        )
        allowed = key_order[None, :] <= query_order[:, None]
        logit_scores = jnp.where(allowed, logit_scores, neg_fill)
        fresh_top = jnp.maximum(top_score, jnp.max(logit_scores, axis=-1))
        weights_now = jnp.where(allowed, jnp.exp(logit_scores - fresh_top[..., None]), 0.0)
        shrink = jnp.exp(top_score - fresh_top)
        weight = weight * shrink + jnp.sum(weights_now, axis=-1)
        mixed_sum = mixed_sum * shrink[..., None] + jnp.einsum(
            "yoih,hyf->yoif",
            weights_now.astype(jnp.bfloat16),
            value_piece,
            preferred_element_type=jnp.float32,
        )
        return (fresh_top, weight, mixed_sum)

    top_score, weight, mixed_sum = lax.fori_loop(0, length // block_rows, one_block, start_state)
    attended = (
        jnp.transpose(mixed_sum / weight[..., None], (2, 0, 1, 3))
        .reshape(rows_here, HEADS * HEAD_DIM)
        .astype(jnp.bfloat16)
    )
    block_out = jnp.dot(
        attended,
        lax.all_gather(w_out, "seq", axis=1, tiled=True),
        preferred_element_type=jnp.float32,
    ).astype(jnp.bfloat16)
    own_compact = jnp.clip(my_start + own_steps, 0, picked_total - 1)
    slot_steps = jnp.arange(slot_count, dtype=jnp.int32)
    lead_back = (my_index - starts) % shards
    offset_back = lead_back[:, None] + shards * slot_steps[None, :]
    valid_back = offset_back < counts[:, None]
    local_k = jnp.clip((starts[:, None] + offset_back - my_index) // shards, 0, ROWS_DEV - 1)
    outgoing_back = jnp.where(
        valid_back[..., None], block_out[local_k], jnp.zeros((), jnp.bfloat16)
    )
    returned = lax.all_to_all(outgoing_back, "seq", split_axis=0, concat_axis=0, tiled=True)
    pick_at = (my_start + own_steps) % shards * slot_count + jnp.clip(
        own_steps // shards, 0, slot_count - 1
    )
    delta_rows = returned.reshape(shards * slot_count, model_width)[pick_at]
    spot_row = jnp.where(own_valid, chosen[own_compact] - my_base, tok_rows)
    lift_rows = gates[own_compact][:, None] * delta_rows.astype(jnp.float32)
    mixed = tokens.astype(jnp.float32).at[spot_row].add(lift_rows, mode="drop")
    return mixed.astype(jnp.bfloat16)


def solution(mesh):
    return jax.shard_map(
        per_device,
        mesh=mesh,
        in_specs=(
            P(("dp", "seq"), None),
            P("dp"),
            P("dp"),
            P("seq", None),
            P("seq", None),
            P("seq", None),
            P(None, "seq"),
        ),
        out_specs=P(("dp", "seq"), None),
        check_vma=False,
    )
```

profile of v0, /device:TPU:0, one launch (start us, length us, event | category | flops | bytes accessed | tf_op | source)
XLA Modules:
  0.0 318.1 jit_solution(3164678104505626016)
XLA Ops:
  6.5 0.7 all-gather.9.cloned.1.call-update
  7.3 0.7 all-gather.5.cloned.1.call-update
  9.3 0.7 add_select_fusion.3
  13.8 1.4 gather_fusion.2
  15.3 5.1 %gather_fusion.3 = bf16[256,2048]{1,0:T(8,128)(2,1)S(1)} fusion(bf16[1024,2048]{1,0:T(8,128)(2,1)} %param.9, s32[1024]{0:T(1024)S(1)} %pad_clamp_fusion.4), kind=kCustom, calls=%fused_computation.3 | custom fusion | bytes 2098176 | tf_op jit(solution)/shard_map/gather | solution.py:45
  20.7 1.3 fusion.21
  22.0 7.3 %all-to-all-start = ((bf16[8,32,2048]{2,1,0:T(8,128)(2,1)}), bf16[8,32,2048]{2,1,0:T(8,128)(2,1)S(1)}, u32[]{:S(2)}, u32[]{:S(2)}) async-start(bf16[8,32,2048]{2,1,0:T(8,128)(2,1)} %fusion.21), calls=%async_computation | async-start | bytes 2097152 | tf_op jit(solution)/shard_map/all_to_all | solution.py:49
  29.3 1.0 gather_fusion.4
  30.5 4.9 %fusion.40 = s32[128]{0:T(128)S(1)} fusion(s32[128]{0:T(128)S(1)} %gather_fusion.4, s32[]{:T(128)} %bitcast.16, s32[]{:T(128)} %bitcast.17, s32[]{:T(128)} %bitcast.18, s32[]{:T(128)} %bitcast.19, s32[]{:T(128)} %bitcast.20, s32[]{:T(128)} %bitcast.22, s32[]{:T(128)} %bitcast.21, s32[]{:T(128)} %bitcast.15, s32[]{:T(128)} %axis_index.12), kind=kLoop, calls=%fused_computation.132 | loop fusion | flops 5120 | bytes 1060 | tf_op jit(solution)/shard_map/select_n | solution.py:54
  35.5 28.1 %all-to-all-done = bf16[8,32,2048]{2,1,0:T(8,128)(2,1)S(1)} async-done(((bf16[8,32,2048]{2,1,0:T(8,128)(2,1)}), bf16[8,32,2048]{2,1,0:T(8,128)(2,1)S(1)}, u32[]{:S(2)}, u32[]{:S(2)}) %all-to-all-start) | async-done | bytes 1048608 | tf_op jit(solution)/shard_map/all_to_all | solution.py:49
  63.5 0.9 gather_fusion.5
  64.5 1.5 convolution_convert_fusion.1
  66.1 32.1 %all_gather.22 = bf16[1024,256]{1,0:T(8,128)(2,1)S(1)} all-gather(bf16[128,256]{1,0:T(8,128)(2,1)S(1)} %convolution_convert_fusion.1), channel_id=1, replica_groups=mesh['dp'=4,'seq'=8] {'seq'}, dimensions={0}, use_global_device_ids=true | all-gather | bytes 589824 | tf_op jit(solution)/shard_map/all_gather | solution.py:81
  98.2 7.5 %all-gather.5.cloned.1.call-done = bf16[2048,256]{1,0:T(8,128)(2,1)} async-done(((bf16[256,256]{1,0:T(8,128)(2,1)}), bf16[2048,256]{1,0:T(8,128)(2,1)}) %all-gather.5.cloned.1.call-update) | async-done | bytes 1048592 | tf_op jit(solution)/shard_map/all_gather | solution.py:62
  105.7 1.5 convolution_convert_fusion.2
  107.2 33.2 %all_gather.19 = bf16[1024,256]{1,0:T(8,128)(2,1)S(1)} all-gather(bf16[128,256]{1,0:T(8,128)(2,1)S(1)} %convolution_convert_fusion.2), channel_id=1, replica_groups=mesh['dp'=4,'seq'=8] {'seq'}, dimensions={0}, use_global_device_ids=true | all-gather | bytes 589824 | tf_op jit(solution)/shard_map/all_gather | solution.py:80
  140.4 42.1 %all-gather.7.cloned.1.call-done = bf16[2048,1024]{1,0:T(8,128)(2,1)} async-done(((bf16[256,1024]{1,0:T(8,128)(2,1)}), bf16[2048,1024]{1,0:T(8,128)(2,1)}) %all-gather.7.cloned.1.call-update) | async-done | bytes 4194320 | tf_op jit(solution)/shard_map/all_gather | solution.py:61
  182.4 2.9 fusion.20
  185.6 4.9 %while.20 = (s32[]{:T(128)}, f32[2,4,128]{2,1,0:T(4,128)S(1)}, f32[2,4,128]{2,1,0:T(4,128)S(1)}, f32[2,4,128,128]{3,2,1,0:T(8,128)S(1)}, bf16[1024,256]{1,0:T(8,...) while((s32[]{:T(128)}, f32[2,4,128]{2,1,0:T(4,128)S(1)}, ...), condition=%wide.region_6.7_spmd.clone, body=%wide.region_3.6_spmd.clone.sunk | while | flops 274153728 | bytes 10556611 | solution.py:112
  187.1 0.9 convolution_add_fusion.2
  189.6 0.9 convolution_add_fusion.2
  190.8 66.8 %all-gather.11.cloned.1.call-done = bf16[1024,2048]{1,0:T(8,128)(2,1)} async-done(((bf16[1024,256]{1,0:T(8,128)(2,1)}), bf16[1024,2048]{1,0:T(8,128)(2,1)}) %all-gather.11.cloned.1.call-update) | async-done | bytes 4194320 | tf_op jit(solution)/shard_map/all_gather | solution.py:120
  257.5 2.9 convolution_convert_fusion
  260.5 1.4 gather_fusion.6
  261.8 1.1 broadcast_select_fusion
  262.9 3.7 %all-to-all-start.1 = ((bf16[8,32,2048]{2,1,0:T(8,128)(2,1)}), bf16[8,32,2048]{2,1,0:T(8,128)(2,1)S(1)}, u32[]{:S(2)}, u32[]{:S(2)}) async-start(bf16[8,32,2048]{2,1,0:T(8,128)(2,1)} %broadcast_select_fusion), calls=%async_computation.1 | async-start | bytes 2097152 | tf_op jit(solution)/shard_map/all_to_all | solution.py:132
  266.7 6.5 %convert_element_type.56 = f32[1024,2048]{1,0:T(8,128)} convert(bf16[1024,2048]{1,0:T(8,128)(2,1)} %param.9) | non-fusion elementwise | flops 2097152 | bytes 12582912 | tf_op jit(solution)/shard_map/convert_element_type | solution.py:139
  273.8 1.4 gather_fusion
  275.2 1.4 gather_fusion.1
  277.3 14.5 %all-to-all-done.1 = bf16[8,32,2048]{2,1,0:T(8,128)(2,1)S(1)} async-done(((bf16[8,32,2048]{2,1,0:T(8,128)(2,1)}), bf16[8,32,2048]{2,1,0:T(8,128)(2,1)S(1)}, u32[]{:S(2)}, u32[]{:S(2)}) %all-to-all-start.1) | async-done | bytes 1048608 | tf_op jit(solution)/shard_map/all_to_all | solution.py:132
  291.7 13.8 %scatter_custom_fusion = f32[1024,2048]{1,0:T(8,128)} fusion(f32[1024,2048]{1,0:T(8,128)} %convert_element_type.56, s32[256]{0:T(256)S(1)} %bitcast.130, f32[256]{0:T(256)S(1)} %gather_fusion.1, bf16[256,2048]{1,0:T(8,128)(2,1)S(1)} %bitcast.120, s32[1024]{0:T(1024)S(1)} %pad_clamp_fusion), kind=kCustom, calls=%fused_computation.43 | custom fusion | flops 1572864 | bytes 9442304 | tf_op jit(solution)/shard_map/scatter-add | solution.py:139
  305.5 6.0 %convert_element_type.70 = bf16[1024,2048]{1,0:T(8,128)(2,1)} convert(f32[1024,2048]{1,0:T(8,128)} %scatter_custom_fusion) | non-fusion elementwise | flops 2097152 | bytes 12582912 | tf_op jit(solution)/shard_map/convert_element_type | solution.py:140
  (70 shorter events, 10.4 us)
Async XLA Ops:
  6.5 268.7 %copy-start = (f32[1024]{0:T(1024)S(1)}, f32[1024]{0:T(1024)}, u32[]{:S(2)}) copy-start(f32[1024]{0:T(1024)} %param.11) | copy-start | bytes 12292
  6.5 7.3 %copy-start.1 = (s32[1024]{0:T(1024)S(1)}, s32[1024]{0:T(1024)}, u32[]{:S(2)}) copy-start(s32[1024]{0:T(1024)} %param.10) | copy-start | bytes 12292
  6.5 58.0 %all-gather.9.cloned.1.call-start = ((), (), s32[]{:S(2)}) async-start(), calls=%async_computation.4 | async-start | bytes 1179648 | tf_op jit(solution)/shard_map/all_gather | solution.py:63
  7.3 98.4 %all-gather.5.cloned.1.call-start = ((), (), s32[]{:S(2)}) async-start(), calls=%async_computation.2 | async-start | bytes 1179648 | tf_op jit(solution)/shard_map/all_gather | solution.py:62
  8.0 174.4 %all-gather.7.cloned.1.call-start = ((), (), s32[]{:S(2)}) async-start(), calls=%async_computation.3 | async-start | bytes 4718592 | tf_op jit(solution)/shard_map/all_gather | solution.py:61
  8.7 248.8 %all-gather.11.cloned.1.call-start = ((), (), s32[]{:S(2)}) async-start(), calls=%async_computation.5 | async-start | bytes 4718592 | tf_op jit(solution)/shard_map/all_gather | solution.py:120
  22.0 41.5 %all-to-all-start = ((bf16[8,32,2048]{2,1,0:T(8,128)(2,1)}), bf16[8,32,2048]{2,1,0:T(8,128)(2,1)S(1)}, u32[]{:S(2)}, u32[]{:S(2)}) async-start(bf16[8,32,2048]{2,1,0:T(8,128)(2,1)} %fusion.21), calls=%async_computation | async-start | bytes 2097152 | tf_op jit(solution)/shard_map/all_to_all | solution.py:49
  262.9 28.8 %all-to-all-start.1 = ((bf16[8,32,2048]{2,1,0:T(8,128)(2,1)}), bf16[8,32,2048]{2,1,0:T(8,128)(2,1)S(1)}, u32[]{:S(2)}, u32[]{:S(2)}) async-start(bf16[8,32,2048]{2,1,0:T(8,128)(2,1)} %broadcast_select_fusion), calls=%async_computation.1 | async-start | bytes 2097152 | tf_op jit(solution)/shard_map/all_to_all | solution.py:132
Sparse Core Ops, SparseCore 0:
  9.5 53.3 all-gather.8
  65.0 40.6 all-gather.4
  107.8 74.5 all-gather.6
  184.3 73.1 all-gather.10
where the time goes:
time: 319 us; the launch traced here: 318 us
  waiting for transfers between devices  161 us (50%)
  blocking collectives  65.3 us (20%)
  other arithmetic  39.7 us (12%)
  local copies, waits for them, and re-layouts  15.1 us (5%)
  between operations  13.4 us (4%)
  matrix products  11.8 us (4%)
  starting transfers between devices  11.1 us (3%)
    all_gather x1, waiting for transfers between devices, per_device(): lax.all_gather(w_out, 'seq', axis=1, tiled=True)  66.8 us
    all_gather x1, waiting for transfers between devices, per_device(): lax.all_gather(w_query, 'seq', axis=0, tiled=True)  42.1 us
    all_gather x1, blocking collectives, per_device(): key_rows = lax.all_gather(keys_all, 'seq', axis=0, tiled=True)  33.2 us
    all_gather x1, blocking collectives, per_device(): value_rows = lax.all_gather(values, 'seq', axis=0, tiled=True)  32.1 us
    all_to_all x1, waiting for transfers between devices, per_device(): lax.all_to_all(outgoing, 'seq', split_axis=0, concat_axis=0, tiled=True)  28.1 us
    all_to_all x1, waiting for transfers between devices, per_device(): lax.all_to_all(outgoing_back, 'seq', split_axis=0, concat_axis=0, tiled=T...  14.5 us
    scatter-add x1, other arithmetic, per_device(): mixed = tokens.astype(jnp.float32).at[spot_row].add(lift_rows, mode='drop')  13.8 us
    all_gather x1, waiting for transfers between devices, per_device(): lax.all_gather(w_key, 'seq', axis=0, tiled=True)  7.47 us
  transfers between devices with their start and end apart: 6, of which 5 were waited for; matrix products, arithmetic and copies ran while one was open for 13% of the time, Pallas kernels for 0%

commit v1 on v0

--- a/solution.py
+++ b/solution.py
@@ -77,8 +77,13 @@
         jnp.zeros((KV_HEADS, group_size, rows_here), jnp.float32),
         jnp.zeros((KV_HEADS, group_size, rows_here, HEAD_DIM), jnp.float32),
     )
-    key_rows = lax.all_gather(keys_all, "seq", axis=0, tiled=True)
-    value_rows = lax.all_gather(values, "seq", axis=0, tiled=True)
+    key_rows, value_rows = jnp.split(
+        lax.all_gather(
+            jnp.concatenate([keys_all, values], axis=1), axis_name="seq", axis=0, tiled=True
+        ),
+        [keys_all.shape[1]],
+        axis=1,
+    )
     length = key_rows.shape[0]
     block_rows = math.gcd(length, 512)
 

time: 319 us -> 356 us (1.12)
  waiting for transfers between devices: 161 us -> 261 us
  blocking collectives: 65.3 us -> 0 us
    all_gather x2 -> x0, blocking collectives: 65.3 us -> none  [the longest x1 33.2 us: per_device(): key_rows = lax.all_gather(keys_all, 'seq', axis=0, tiled=True)]
    all_gather x0 -> x1, waiting for transfers between devices: none -> 37.8 us  [per_device(): lax.all_gather(jnp.concatenate([keys_all, values], axis=1), axis_name='se...]
    all_gather x1, waiting for transfers between devices: 7.47 us -> 39.4 us  [per_device(): lax.all_gather(w_key, 'seq', axis=0, tiled=True)]
    all_gather x1, waiting for transfers between devices: 42.1 us -> 72.2 us  [per_device(): lax.all_gather(w_query, 'seq', axis=0, tiled=True)]
  transfers between devices with their start and end apart: 6 -> 7, of which waited for: 5 -> 6; matrix products, arithmetic and copies ran while one was open for 13% -> 12% of each run, Pallas kernels for 0% -> 0%
where the time goes in v1:
time: 356 us; the launch traced here: 355 us
  waiting for transfers between devices  261 us (73%)
  other arithmetic  40.4 us (11%)
  local copies, waits for them, and re-layouts  16.9 us (5%)
  between operations  13.4 us (4%)
  matrix products  11.7 us (3%)
  starting transfers between devices  11.2 us (3%)
    all_gather x1, waiting for transfers between devices, per_device(): lax.all_gather(w_query, 'seq', axis=0, tiled=True)  72.2 us
    all_gather x1, waiting for transfers between devices, per_device(): lax.all_gather(w_out, 'seq', axis=1, tiled=True)  66.8 us
    all_gather x1, waiting for transfers between devices, per_device(): lax.all_gather(w_key, 'seq', axis=0, tiled=True)  39.4 us
    all_gather x1, waiting for transfers between devices, per_device(): lax.all_gather(jnp.concatenate([keys_all, values], axis=1), axis_name='se...  37.8 us
    all_to_all x1, waiting for transfers between devices, per_device(): lax.all_to_all(outgoing, 'seq', split_axis=0, concat_axis=0, tiled=True)  28.1 us
    all_to_all x1, waiting for transfers between devices, per_device(): lax.all_to_all(outgoing_back, 'seq', split_axis=0, concat_axis=0, tiled=T...  14.5 us
    scatter-add x1, other arithmetic, per_device(): mixed = tokens.astype(jnp.float32).at[spot_row].add(lift_rows, mode='drop')  13.7 us
    all_to_all x1, starting transfers between devices, per_device(): lax.all_to_all(outgoing, 'seq', split_axis=0, concat_axis=0, tiled=True)  7.28 us
  transfers between devices with their start and end apart: 7, of which 6 were waited for; matrix products, arithmetic and copies ran while one was open for 12% of the time, Pallas kernels for 0%

profile of v1, /device:TPU:0, one launch (start us, length us, event | category | flops | bytes accessed | tf_op | source)
XLA Modules:
  0.0 355.0 jit_solution(16705344098729269317)
XLA Ops:
  6.5 0.7 all-gather.8.cloned.1.call-update
  7.3 0.7 add_select_fusion.3
  10.2 0.7 fusion.23
  11.8 1.9 gather_fusion.2
  13.8 5.1 %gather_fusion.3 = bf16[256,2048]{1,0:T(8,128)(2,1)S(1)} fusion(bf16[1024,2048]{1,0:T(8,128)(2,1)} %param.9, s32[1024]{0:T(1024)S(1)} %pad_clamp_fusion.4), kind=kCustom, calls=%fused_computation.3 | custom fusion | bytes 2098176 | tf_op jit(solution)/shard_map/gather | solution.py:45
  19.2 1.3 fusion.21
  20.5 7.3 %all-to-all-start = ((bf16[8,32,2048]{2,1,0:T(8,128)(2,1)}), bf16[8,32,2048]{2,1,0:T(8,128)(2,1)S(1)}, u32[]{:S(2)}, u32[]{:S(2)}) async-start(bf16[8,32,2048]{2,1,0:T(8,128)(2,1)} %fusion.21), calls=%async_computation | async-start | bytes 2097152 | tf_op jit(solution)/shard_map/all_to_all | solution.py:49
  28.6 1.0 gather_fusion.4
  29.6 4.9 %fusion.40 = s32[128]{0:T(128)S(1)} fusion(s32[128]{0:T(128)S(1)} %gather_fusion.4, s32[]{:T(128)} %bitcast.16, s32[]{:T(128)} %bitcast.17, s32[]{:T(128)} %bitcast.18, s32[]{:T(128)} %bitcast.19, s32[]{:T(128)} %bitcast.20, s32[]{:T(128)} %bitcast.22, s32[]{:T(128)} %bitcast.21, s32[]{:T(128)} %bitcast.15, s32[]{:T(128)} %axis_index.12), kind=kLoop, calls=%fused_computation.133 | loop fusion | flops 5120 | bytes 1060 | tf_op jit(solution)/shard_map/select_n | solution.py:54
  34.5 28.1 %all-to-all-done = bf16[8,32,2048]{2,1,0:T(8,128)(2,1)S(1)} async-done(((bf16[8,32,2048]{2,1,0:T(8,128)(2,1)}), bf16[8,32,2048]{2,1,0:T(8,128)(2,1)S(1)}, u32[]{:S(2)}, u32[]{:S(2)}) %all-to-all-start) | async-done | bytes 1048608 | tf_op jit(solution)/shard_map/all_to_all | solution.py:49
  62.7 0.9 gather_fusion.5
  63.6 1.5 convolution_convert_fusion.1
  65.2 39.4 %all-gather.6.cloned.1.call-done = bf16[2048,256]{1,0:T(8,128)(2,1)} async-done(((bf16[256,256]{1,0:T(8,128)(2,1)}), bf16[2048,256]{1,0:T(8,128)(2,1)}) %all-gather.6.cloned.1.call-update) | async-done | bytes 1048592 | tf_op jit(solution)/shard_map/all_gather | solution.py:62
  104.5 1.5 convolution_convert_fusion.2
  108.1 37.8 %all-gather.10.cloned.1.call-done = bf16[1024,512]{1,0:T(8,128)(2,1)} async-done(((bf16[128,512]{1,0:T(8,128)(2,1)}), bf16[1024,512]{1,0:T(8,128)(2,1)}) %all-gather.10.cloned.1.call-update) | async-done | bytes 1048592 | tf_op jit(solution)/shard_map/all_gather | solution.py:81
  145.9 1.3 fusion.43
  147.2 72.2 %all-gather.12.cloned.1.call-done = bf16[2048,1024]{1,0:T(8,128)(2,1)} async-done(((bf16[256,1024]{1,0:T(8,128)(2,1)}), bf16[2048,1024]{1,0:T(8,128)(2,1)}) %all-gather.12.cloned.1.call-update) | async-done | bytes 4194320 | tf_op jit(solution)/shard_map/all_gather | solution.py:61
  219.4 2.9 fusion.20
  222.6 4.9 %while.20 = (s32[]{:T(128)}, f32[2,4,128]{2,1,0:T(4,128)S(1)}, f32[2,4,128]{2,1,0:T(4,128)S(1)}, f32[2,4,128,128]{3,2,1,0:T(8,128)S(1)}, bf16[1024,256]{1,0:T(8,...) while((s32[]{:T(128)}, f32[2,4,128]{2,1,0:T(4,128)S(1)}, ...), condition=%wide.region_6.7_spmd.clone, body=%wide.region_3.6_spmd.clone.sunk | while | flops 274153728 | bytes 10556611 | solution.py:117
  224.1 0.9 convolution_add_fusion.2
  226.6 0.9 convolution_add_fusion.2
  227.7 66.8 %all-gather.14.cloned.1.call-done = bf16[1024,2048]{1,0:T(8,128)(2,1)} async-done(((bf16[1024,256]{1,0:T(8,128)(2,1)}), bf16[1024,2048]{1,0:T(8,128)(2,1)}) %all-gather.14.cloned.1.call-update) | async-done | bytes 4194320 | tf_op jit(solution)/shard_map/all_gather | solution.py:125
  294.5 2.9 convolution_convert_fusion
  297.5 1.4 gather_fusion.6
  298.8 1.1 broadcast_select_fusion
  299.9 3.7 %all-to-all-start.1 = ((bf16[8,32,2048]{2,1,0:T(8,128)(2,1)}), bf16[8,32,2048]{2,1,0:T(8,128)(2,1)S(1)}, u32[]{:S(2)}, u32[]{:S(2)}) async-start(bf16[8,32,2048]{2,1,0:T(8,128)(2,1)} %broadcast_select_fusion), calls=%async_computation.1 | async-start | bytes 2097152 | tf_op jit(solution)/shard_map/all_to_all | solution.py:137
  303.7 6.5 %convert_element_type.56 = f32[1024,2048]{1,0:T(8,128)} convert(bf16[1024,2048]{1,0:T(8,128)(2,1)} %param.9) | non-fusion elementwise | flops 2097152 | bytes 12582912 | tf_op jit(solution)/shard_map/convert_element_type | solution.py:144
  310.9 1.4 gather_fusion
  312.2 1.4 gather_fusion.1
  314.3 14.5 %all-to-all-done.1 = bf16[8,32,2048]{2,1,0:T(8,128)(2,1)S(1)} async-done(((bf16[8,32,2048]{2,1,0:T(8,128)(2,1)}), bf16[8,32,2048]{2,1,0:T(8,128)(2,1)S(1)}, u32[]{:S(2)}, u32[]{:S(2)}) %all-to-all-start.1) | async-done | bytes 1048608 | tf_op jit(solution)/shard_map/all_to_all | solution.py:137
  328.7 13.7 %scatter_custom_fusion = f32[1024,2048]{1,0:T(8,128)} fusion(f32[1024,2048]{1,0:T(8,128)} %convert_element_type.56, s32[256]{0:T(256)S(1)} %bitcast.130, f32[256]{0:T(256)S(1)} %gather_fusion.1, bf16[256,2048]{1,0:T(8,128)(2,1)S(1)} %bitcast.120, s32[1024]{0:T(1024)S(1)} %pad_clamp_fusion), kind=kCustom, calls=%fused_computation.43 | custom fusion | flops 1572864 | bytes 9442304 | tf_op jit(solution)/shard_map/scatter-add | solution.py:144
  342.5 6.0 %convert_element_type.70 = bf16[1024,2048]{1,0:T(8,128)(2,1)} convert(f32[1024,2048]{1,0:T(8,128)} %scatter_custom_fusion) | non-fusion elementwise | flops 2097152 | bytes 12582912 | tf_op jit(solution)/shard_map/convert_element_type | solution.py:145
  (73 shorter events, 11.0 us)
Async XLA Ops:
  6.5 305.7 %copy-start = (f32[1024]{0:T(1024)S(1)}, f32[1024]{0:T(1024)}, u32[]{:S(2)}) copy-start(f32[1024]{0:T(1024)} %param.11) | copy-start | bytes 12292
  6.5 57.1 %all-gather.8.cloned.1.call-start = ((), (), s32[]{:S(2)}) async-start(), calls=%async_computation.3 | async-start | bytes 1179648 | tf_op jit(solution)/shard_map/all_gather | solution.py:63
  20.5 42.1 %all-to-all-start = ((bf16[8,32,2048]{2,1,0:T(8,128)(2,1)}), bf16[8,32,2048]{2,1,0:T(8,128)(2,1)S(1)}, u32[]{:S(2)}, u32[]{:S(2)}) async-start(bf16[8,32,2048]{2,1,0:T(8,128)(2,1)} %fusion.21), calls=%async_computation | async-start | bytes 2097152 | tf_op jit(solution)/shard_map/all_to_all | solution.py:49
  27.8 76.7 %all-gather.6.cloned.1.call-start = ((), (), s32[]{:S(2)}) async-start(), calls=%async_computation.2 | async-start | bytes 1179648 | tf_op jit(solution)/shard_map/all_gather | solution.py:62
  28.5 117.4 %all-gather.10.cloned.1.call-start = ((), (), s32[]{:S(2)}) async-start(), calls=%async_computation.4 | async-start | bytes 1179648 | tf_op jit(solution)/shard_map/all_gather | solution.py:81
  106.8 112.7 %all-gather.12.cloned.1.call-start = ((), (), s32[]{:S(2)}) async-start(), calls=%async_computation.5 | async-start | bytes 4718592 | tf_op jit(solution)/shard_map/all_gather | solution.py:61
  107.4 187.2 %all-gather.14.cloned.1.call-start = ((), (), s32[]{:S(2)}) async-start(), calls=%async_computation.6 | async-start | bytes 4718592 | tf_op jit(solution)/shard_map/all_gather | solution.py:125
  299.9 28.8 %all-to-all-start.1 = ((bf16[8,32,2048]{2,1,0:T(8,128)(2,1)}), bf16[8,32,2048]{2,1,0:T(8,128)(2,1)S(1)}, u32[]{:S(2)}, u32[]{:S(2)}) async-start(bf16[8,32,2048]{2,1,0:T(8,128)(2,1)} %broadcast_select_fusion), calls=%async_computation.1 | async-start | bytes 2097152 | tf_op jit(solution)/shard_map/all_to_all | solution.py:137
  303.7 7.2 %copy-start.1 = (s32[1024]{0:T(1024)S(1)}, s32[1024]{0:T(1024)}, u32[]{:S(2)}) copy-start(s32[1024]{0:T(1024)} %param.10) | copy-start | bytes 12292
Sparse Core Ops, SparseCore 0:
  9.5 52.9 all-gather.7
  64.6 39.8 all-gather.5
  106.9 38.9 all-gather.9
  147.9 71.4 all-gather.11
  221.3 73.1 all-gather.13
